TPU v7x, 32 devices: a whole 2x2x4 slice. The times are simulated.
32 devices in a mesh: gx: 8 (over z, core), gz: 4 (over y, x).
Axes of the slice: x: 2, y: 2, z: 4, core: 2. Of those that a mesh axis runs over, the one named last changes fastest.
Arguments:
- populations: float32 [19, 8, 32, 1024], P(None, None, 'gz', 'gx'), may hold values from 0.001 to 0.6, as said below
- solid: int32 [8, 32, 1024], P(None, 'gz', 'gx'), may hold values from 0 to 1, as said below
- top_inflow: float32 [5, 32, 1024], P(None, 'gz', 'gx'), may hold values from 0.005 to 0.1
Outputs:
- advanced: float32 [19, 8, 32, 1024], P(None, None, 'gz', 'gx')
Inputs may be any that keep to these rules, and one draw needn't show every extreme that they name: Positive populations near equilibrium. Only the two planes nearest the wall hold solid nodes.
All inputs are finite; a program needn't handle non-finite values.
Results may differ from a plain program's by a relative error of at most 0.0003.
Values sent between devices are 32-bit elements; how exact they have to be, the bound alone decides.
A program may use at most 64 MiB of HBM per device.

v0:
```python
from functools import reduce
import jax
import jax.numpy as jnp
import numpy as np
from jax import lax
from jax.sharding import PartitionSpec as P

STEPS = 2
lattice = np.array(
    [
        [0, 0, 0],
        [1, 0, 0],
        [-1, 0, 0],
        [0, 1, 0],
        [0, -1, 0],
        [0, 0, 1],
        [0, 0, -1],
        [1, 1, 0],
        [-1, -1, 0],
        [1, -1, 0],
        [-1, 1, 0],
        [1, 0, 1],
        [-1, 0, -1],
        [1, 0, -1],
        [-1, 0, 1],
        [0, 1, 1],
        [0, -1, -1],
        [0, 1, -1],
        [0, -1, 1],
    ]
)
lattice_weights = [1.0 / 3.0] + [1.0 / 18.0] * 6 + [1.0 / 36.0] * 12
opposite = [0, 2, 1, 4, 3, 6, 5, 8, 7, 10, 9, 12, 11, 14, 13, 16, 15, 18, 17]
incoming = [4, 8, 9, 16, 18]
base_drive = 0.0001
drive_gain = 1.0
target_flow = 0.1


def extended(block, sides, width):
    for axis, dim in sides:
        count = lax.axis_size(axis)
        forward = [(i, i + 1) for i in range(count - 1)]
        forward.append((count - 1, 0))
        backward = [(target, source) for source, target in forward]
        low = lax.ppermute(
            lax.slice_in_dim(block, block.shape[dim] - width, None, axis=dim), axis, forward
        )
        high = lax.ppermute(lax.slice_in_dim(block, 0, width, axis=dim), axis, backward)
        block = jnp.concatenate([low, block, high], axis=dim)
    return block


def invert_rows(matrix):
    order = len(matrix)
    work = [
        list(matrix[row]) + [1.0 if col == row else 0.0 for col in range(order)]
        for row in range(order)
    ]
    for col in range(order):
        pivot = max(range(col, order), key=lambda row: abs(work[row][col]))
        work[col], work[pivot] = (work[pivot], work[col])
        lead = work[col][col]
        work[col] = [value / lead for value in work[col]]
        for row in range(order):
            if row != col:
                factor = work[row][col]
                if factor != 0.0:
                    work[row] = [
                        value - factor * other for value, other in zip(work[row], work[col])
                    ]
    return [line[order:] for line in work]


def collide_matrix():
    moment_rows = []
    for power in [
        (0, 0, 0),
        (1, 0, 0),
        (0, 1, 0),
        (0, 0, 1),
        (1, 1, 0),
        (1, 0, 1),
        (0, 1, 1),
        (2, 0, 0),
        (0, 2, 0),
        (0, 0, 2),
        (1, 2, 0),
        (1, 0, 2),
        (2, 1, 0),
        (0, 1, 2),
        (2, 0, 1),
        (0, 2, 1),
        (2, 2, 0),
        (2, 0, 2),
        (0, 2, 2),
    ]:
        moment_rows.append(
            [
                float(
                    int(lattice[q, 0]) ** power[0]
                    * int(lattice[q, 1]) ** power[1]
                    * int(lattice[q, 2]) ** power[2]
                )
                for q in range(19)
            ]
        )
    rates = [0.0] * 4 + [1.8] * 6 + [1.2] * 6 + [1.1] * 3
    inverse = invert_rows(moment_rows)
    result = [
        [
            sum((inverse[row][mid] * rates[mid] * moment_rows[mid][col] for mid in range(19)))
            for col in range(19)
        ]
        for row in range(19)
    ]
    return np.array(result, dtype=np.float32)


def signed_sum(populations, component):
    plus_terms = [populations[index] for index in range(19) if lattice[index, component] == 1]
    minus_terms = [populations[index] for index in range(19) if lattice[index, component] == -1]
    return reduce(lambda left, right: left + right, plus_terms) - reduce(
        lambda left, right: left + right, minus_terms
    )


def moments(populations):
    density = jnp.sum(populations, axis=0)
    momentum = (signed_sum(populations, 0), signed_sum(populations, 1), signed_sum(populations, 2))
    return (density, momentum)


def project(index, velocity):
    result = jnp.zeros_like(velocity[0])
    for component in range(3):
        factor = int(lattice[index, component])
        if factor == 1:
            result = result + velocity[component]
        elif factor == -1:
            result = result - velocity[component]
    return result


def equilibrium(density, velocity):
    speed_square = velocity[0] * velocity[0] + velocity[1] * velocity[1] + velocity[2] * velocity[2]
    terms = []
    for index in range(19):
        along = project(index, velocity)
        terms.append(
            lattice_weights[index]
            * density
            * (1.0 + 3.0 * along + 4.5 * along * along - 1.5 * speed_square)
        )
    return jnp.stack(terms)


def collide(current, density, momentum, driving):
    velocity = tuple((part_value / density for part_value in momentum))
    base_state = equilibrium(density, velocity)
    pushed = equilibrium(density, (velocity[0] + driving / density, velocity[1], velocity[2]))
    relaxed = jnp.tensordot(
        jnp.asarray(collide_matrix()), current - base_state, axes=1, precision=lax.Precision.HIGHEST
    )
    return current - relaxed + pushed - base_state


def extend(collided):
    return extended(collided, (("gx", 3), ("gz", 2)), 1)


def shift_planes(carried, blocked, step_y):
    if step_y == 1:
        carried = jnp.concatenate([jnp.zeros_like(carried[:1]), carried[:-1]], axis=0)
        blocked = jnp.concatenate([jnp.ones_like(blocked[:1]), blocked[:-1]], axis=0)
    elif step_y == -1:
        carried = jnp.concatenate([carried[1:], jnp.zeros_like(carried[:1])], axis=0)
        blocked = jnp.concatenate([blocked[1:], jnp.zeros_like(blocked[:1])], axis=0)
    return (carried, blocked)


def trim(array, cut):
    if cut == 0:
        return array
    return array[..., cut:-cut, cut:-cut]


def stream_block(padded, solid_padded, top_inflow, before):
    planes = padded.shape[1]
    width_z = padded.shape[2] - 2
    width_x = padded.shape[3] - 2
    collided = trim(padded, 1)
    solid = trim(solid_padded, 1)
    results = []
    for index in range(19):
        step_x = int(lattice[index, 0])
        step_y = int(lattice[index, 1])
        step_z = int(lattice[index, 2])
        carried = padded[
            index, :, 1 - step_z : 1 - step_z + width_z, 1 - step_x : 1 - step_x + width_x
        ]
        blocked = solid_padded[
            :, 1 - step_z : 1 - step_z + width_z, 1 - step_x : 1 - step_x + width_x
        ]
        carried, blocked = shift_planes(carried, blocked, step_y)
        arrived = jnp.where(blocked == 1, collided[opposite[index]], carried)
        if step_y == -1:
            arrived = arrived.at[planes - 1].set(top_inflow[incoming.index(index)])
        results.append(arrived)
    return jnp.where(solid[None] == 1, before, jnp.stack(results))


def total_flow(local_sum, node_total):
    return lax.psum(local_sum, ("gx", "gz")) / node_total


def local(populations, solid, top_inflow):
    node_total = float(
        populations.shape[1]
        * populations.shape[2]
        * populations.shape[3]
        * lax.axis_size("gx")
        * lax.axis_size("gz")
    )
    fluid_nodes = (1 - solid).astype(jnp.float32)
    solid_padded = extended(solid, (("gx", 2), ("gz", 1)), 1)
    current = populations
    for step_index in range(STEPS):
        density, momentum = moments(current)
        local_sum = jnp.sum(momentum[0] * fluid_nodes)
        bulk_flow = total_flow(local_sum, node_total)
        driving = base_drive + drive_gain * (target_flow - bulk_flow)
        collided = collide(current, density, momentum, driving)
        padded = extend(collided)
        current = stream_block(padded, solid_padded, top_inflow, current)
    return current


def solution(mesh):
    return jax.shard_map(
        local,
        mesh=mesh,
        in_specs=(P(None, None, "gz", "gx"), P(None, "gz", "gx"), P(None, "gz", "gx")),
        out_specs=P(None, None, "gz", "gx"),
        check_vma=False,
    )
```

profile of v0, /device:TPU:0, one launch (start us, length us, event | category | flops | bytes accessed | tf_op | source)
XLA Modules:
  0.0 149.5 jit_solution(2305365441169737833)
XLA Ops:
  0.0 1.0 fusion.266
  1.0 4.5 %collective-permute-start.2 = (s32[8,8,1]{2,1,0:T(8,128)S(1)}, s32[8,8,1]{2,1,0:T(8,128)S(1)}, u32[]{:S(2)}, u32[]{:S(2)}) collective-permute-start(s32[8,8,1]{2,1,0:T(8,128)S(1)} %get-tuple-element.284), channel_id=1, source_target_pairs={{4,0},{8,4},{12,8},{16,12},{20,16},{24,20},{28,24},{0,28},{5,1},{9... | collective-permute-start | bytes 776 | tf_op jit(solution)/shard_map/ppermute | solution.py:49
  5.5 1.5 %fusion.243 = (f32[]{:T(128)}, f32[1,8,8,128]{3,2,1,0:T(8,128)S(1)}) fusion(s32[8,8,128]{2,1,0:T(8,128)S(1)} %copy-done.1, f32[19,8,8,128]{3,2,1,0:T(8,128)} %param.25), kind=kLoop, calls=%fused_computation.503 | loop fusion | flops 106495 | bytes 393220 | tf_op jit(solution)/shard_map/reduce_sum | solution.py:230
  7.0 1.1 reduce_sum.40
  8.2 39.1 %psum.14 = f32[]{:T(128)} all-reduce(f32[]{:T(128)} %get-tuple-element.179), channel_id=1, replica_groups=mesh['gx'=8,'gz'=4] {'gx','gz'}, use_global_device_ids=true, to_apply=%region_2.0 | all-reduce | flops 1 | bytes 8 | tf_op jit(solution)/shard_map/psum | solution.py:214
  49.4 1.1 fusion.2
  50.9 1.2 copy.80
  52.6 3.6 %collective-permute-start.3 = (f32[19,8,8,1]{0,2,3,1:T(8,128)S(1)}, f32[19,8,8,1]{0,2,3,1:T(8,128)S(1)}, u32[]{:S(2)}, u32[]{:S(2)}) collective-permute-start(f32[19,8,8,1]{0,2,3,1:T(8,128)S(1)} %copy.82), channel_id=1, source_target_pairs={{4,0},{8,4},{12,8},{16,12},{20,16},{24,20},{28,24},{0,28},{5,1},{9... | collective-permute-start | bytes 14600 | tf_op jit(solution)/shard_map/ppermute | solution.py:49
  56.4 3.4 %collective-permute-start.6 = (s32[8,1,130]{2,1,0:T(1,128)S(1)}, s32[8,1,130]{2,1,0:T(1,128)S(1)}, u32[]{:S(2)}, u32[]{:S(2)}) collective-permute-start(s32[8,1,130]{2,1,0:T(1,128)S(1)} %get-tuple-element.242), channel_id=1, source_target_pairs={{1,0},{2,1},{3,2},{0,3},{5,4},{6,5},{7,6},{4,7},{9,8},{10,9},{11,1... | collective-permute-start | bytes 12488 | tf_op jit(solution)/shard_map/ppermute | solution.py:49
  59.8 0.7 pad_add_fusion.1
  60.5 0.7 fusion.265
  61.2 3.1 %collective-permute-done.4 = s32[8,1,130]{2,1,0:T(1,128)S(1)} collective-permute-done((s32[8,1,130]{2,1,0:T(1,128)S(1)}, s32[8,1,130]{2,1,0:T(1,128)S(1)}, u32[]{:S(2)}, u32[]{:S(2)}) %collective-permute-start.4) | collective-permute-done | bytes 4192 | tf_op jit(solution)/shard_map/ppermute | solution.py:46
  64.4 0.7 fusion.263
  65.2 0.7 copy.83
  65.9 1.5 copy.81
  67.5 1.0 pad_maximum_fusion.3
  69.3 2.0 %collective-permute-start.5 = (f32[19,8,1,130]{3,2,1,0:T(1,128)S(1)}, f32[19,8,1,130]{3,2,1,0:T(1,128)S(1)}, u32[]{:S(2)}, u32[]{:S(2)}) collective-permute-start(f32[19,8,1,130]{3,2,1,0:T(1,128)S(1)} %get-tuple-element.198), channel_id=1, source_target_pairs={{0,1},{1,2},{2,3},{3,0},{4,5},{5,6},{6,7},{7,4},{8,9},{9,10},{10,1... | collective-permute-start | bytes 237128 | tf_op jit(solution)/shard_map/ppermute | solution.py:46
  71.9 2.6 %collective-permute-done.7 = f32[19,8,1,130]{3,2,1,0:T(1,128)S(1)} collective-permute-done((f32[19,8,1,130]{3,2,1,0:T(1,128)S(1)}, f32[19,8,1,130]{3,2,1,0:T(1,128)S(1)}, u32[]{:S(2)}, u32[]{:S(2)}) %collective-permute-start.7) | collective-permute-done | bytes 79072 | tf_op jit(solution)/shard_map/ppermute | solution.py:49
  74.5 1.5 %collective-permute-done.5 = f32[19,8,1,130]{3,2,1,0:T(1,128)S(1)} collective-permute-done((f32[19,8,1,130]{3,2,1,0:T(1,128)S(1)}, f32[19,8,1,130]{3,2,1,0:T(1,128)S(1)}, u32[]{:S(2)}, u32[]{:S(2)}) %collective-permute-start.5) | collective-permute-done | bytes 79072 | tf_op jit(solution)/shard_map/ppermute | solution.py:46
  79.6 0.7 copy-done.5
  82.1 0.7 copy-done.3
  83.5 38.8 %psum.15 = f32[]{:T(128)} all-reduce(f32[]{:T(128)} %get-tuple-element.131), channel_id=1, replica_groups=mesh['gx'=8,'gz'=4] {'gx','gz'}, use_global_device_ids=true, to_apply=%region_5.6 | all-reduce | flops 1 | bytes 8 | tf_op jit(solution)/shard_map/psum | solution.py:214
  124.5 1.1 fusion
  127.2 3.5 %collective-permute-start.9 = (f32[19,8,8,1]{0,2,3,1:T(8,128)S(1)}, f32[19,8,8,1]{0,2,3,1:T(8,128)S(1)}, u32[]{:S(2)}, u32[]{:S(2)}) collective-permute-start(f32[19,8,8,1]{0,2,3,1:T(8,128)S(1)} %copy.90), channel_id=1, source_target_pairs={{4,0},{8,4},{12,8},{16,12},{20,16},{24,20},{28,24},{0,28},{5,1},{9... | collective-permute-start | bytes 14600 | tf_op jit(solution)/shard_map/ppermute | solution.py:49
  131.3 1.0 collective-permute-done.9
  132.3 0.7 copy.91
  133.0 0.7 copy.89
  133.9 1.0 pad_maximum_fusion
  134.9 3.6 %collective-permute-start.11 = (f32[19,8,1,130]{3,2,1,0:T(1,128)S(1)}, f32[19,8,1,130]{3,2,1,0:T(1,128)S(1)}, u32[]{:S(2)}, u32[]{:S(2)}) collective-permute-start(f32[19,8,1,130]{3,2,1,0:T(1,128)S(1)} %get-tuple-element.193), channel_id=1, source_target_pairs={{1,0},{2,1},{3,2},{0,3},{5,4},{6,5},{7,6},{4,7},{9,8},{10,9},{11,1... | collective-permute-start | bytes 237128 | tf_op jit(solution)/shard_map/ppermute | solution.py:49
  139.9 3.0 %collective-permute-done.11 = f32[19,8,1,130]{3,2,1,0:T(1,128)S(1)} collective-permute-done((f32[19,8,1,130]{3,2,1,0:T(1,128)S(1)}, f32[19,8,1,130]{3,2,1,0:T(1,128)S(1)}, u32[]{:S(2)}, u32[]{:S(2)}) %collective-permute-start.11) | collective-permute-done | bytes 79072 | tf_op jit(solution)/shard_map/ppermute | solution.py:49
  142.9 2.8 %collective-permute-done.10 = f32[19,8,1,130]{3,2,1,0:T(1,128)S(1)} collective-permute-done((f32[19,8,1,130]{3,2,1,0:T(1,128)S(1)}, f32[19,8,1,130]{3,2,1,0:T(1,128)S(1)}, u32[]{:S(2)}, u32[]{:S(2)}) %collective-permute-start.10) | collective-permute-done | bytes 79072 | tf_op jit(solution)/shard_map/ppermute | solution.py:46
  148.5 0.9 broadcast_select_fusion
  (170 shorter events, 17.7 us)
Async XLA Ops:
  0.0 5.5 %copy-start.1 = (s32[8,8,128]{2,1,0:T(8,128)S(1)}, s32[8,8,128]{2,1,0:T(8,128)}, u32[]{:S(2)}) copy-start(s32[8,8,128]{2,1,0:T(8,128)} %param.26) | copy-start | bytes 98308
  0.0 47.9 %copy-start = (f32[19,8,8,128]{3,2,1,0:T(8,128)S(1)}, f32[19,8,8,128]{3,2,1,0:T(8,128)}, u32[]{:S(2)}) copy-start(f32[19,8,8,128]{3,2,1,0:T(8,128)} %param.25) | copy-start | bytes 1867780
  1.0 55.3 %collective-permute-start.2 = (s32[8,8,1]{2,1,0:T(8,128)S(1)}, s32[8,8,1]{2,1,0:T(8,128)S(1)}, u32[]{:S(2)}, u32[]{:S(2)}) collective-permute-start(s32[8,8,1]{2,1,0:T(8,128)S(1)} %get-tuple-element.284), channel_id=1, source_target_pairs={{4,0},{8,4},{12,8},{16,12},{20,16},{24,20},{28,24},{0,28},{5,1},{9... | collective-permute-start | bytes 776 | tf_op jit(solution)/shard_map/ppermute | solution.py:49
  5.5 50.7 %collective-permute-start = (s32[8,8,1]{2,1,0:T(8,128)S(1)}, s32[8,8,1]{2,1,0:T(8,128)S(1)}, u32[]{:S(2)}, u32[]{:S(2)}) collective-permute-start(s32[8,8,1]{2,1,0:T(8,128)S(1)} %get-tuple-element.285), channel_id=1, source_target_pairs={{0,4},{4,8},{8,12},{12,16},{16,20},{20,24},{24,28},{28,0},{1,5},{5... | collective-permute-start | bytes 776 | tf_op jit(solution)/shard_map/ppermute | solution.py:46
  48.7 0.7 copy-start.14
  52.1 13.8 %collective-permute-start.1 = (f32[19,8,8,1]{0,2,3,1:T(8,128)}, f32[19,8,8,1]{0,2,3,1:T(8,128)}, u32[]{:S(2)}, u32[]{:S(2)}) collective-permute-start(f32[19,8,8,1]{0,2,3,1:T(8,128)} %copy.80), channel_id=1, source_target_pairs={{0,4},{4,8},{8,12},{12,16},{16,20},{20,24},{24,28},{28,0},{1,5},{5... | collective-permute-start | bytes 14600 | tf_op jit(solution)/shard_map/ppermute | solution.py:46
  52.6 12.6 %collective-permute-start.3 = (f32[19,8,8,1]{0,2,3,1:T(8,128)S(1)}, f32[19,8,8,1]{0,2,3,1:T(8,128)S(1)}, u32[]{:S(2)}, u32[]{:S(2)}) collective-permute-start(f32[19,8,8,1]{0,2,3,1:T(8,128)S(1)} %copy.82), channel_id=1, source_target_pairs={{4,0},{8,4},{12,8},{16,12},{20,16},{24,20},{28,24},{0,28},{5,1},{9... | collective-permute-start | bytes 14600 | tf_op jit(solution)/shard_map/ppermute | solution.py:49
  56.4 4.8 %collective-permute-start.6 = (s32[8,1,130]{2,1,0:T(1,128)S(1)}, s32[8,1,130]{2,1,0:T(1,128)S(1)}, u32[]{:S(2)}, u32[]{:S(2)}) collective-permute-start(s32[8,1,130]{2,1,0:T(1,128)S(1)} %get-tuple-element.242), channel_id=1, source_target_pairs={{1,0},{2,1},{3,2},{0,3},{5,4},{6,5},{7,6},{4,7},{9,8},{10,9},{11,1... | collective-permute-start | bytes 12488 | tf_op jit(solution)/shard_map/ppermute | solution.py:49
  59.7 4.5 %collective-permute-start.4 = (s32[8,1,130]{2,1,0:T(1,128)S(1)}, s32[8,1,130]{2,1,0:T(1,128)S(1)}, u32[]{:S(2)}, u32[]{:S(2)}) collective-permute-start(s32[8,1,130]{2,1,0:T(1,128)S(1)} %get-tuple-element.243), channel_id=1, source_target_pairs={{0,1},{1,2},{2,3},{3,0},{4,5},{5,6},{6,7},{7,4},{8,9},{9,10},{10,1... | collective-permute-start | bytes 12488 | tf_op jit(solution)/shard_map/ppermute | solution.py:46
  68.6 2.7 %copy-start.12 = (s32[7,8,128]{2,1,0:T(8,128)S(1)}, s32[7,8,128]{2,1,0:T(8,128)}, u32[]{:S(2)}) copy-start(s32[7,8,128]{2,1,0:T(8,128)} %get-tuple-element.282) | copy-start | bytes 86020
  69.3 5.2 %collective-permute-start.7 = (f32[19,8,1,130]{3,2,1,0:T(1,128)S(1)}, f32[19,8,1,130]{3,2,1,0:T(1,128)S(1)}, u32[]{:S(2)}, u32[]{:S(2)}) collective-permute-start(f32[19,8,1,130]{3,2,1,0:T(1,128)S(1)} %get-tuple-element.197), channel_id=1, source_target_pairs={{1,0},{2,1},{3,2},{0,3},{5,4},{6,5},{7,6},{4,7},{9,8},{10,9},{11,1... | collective-permute-start | bytes 237128 | tf_op jit(solution)/shard_map/ppermute | solution.py:49
  69.3 6.7 %collective-permute-start.5 = (f32[19,8,1,130]{3,2,1,0:T(1,128)S(1)}, f32[19,8,1,130]{3,2,1,0:T(1,128)S(1)}, u32[]{:S(2)}, u32[]{:S(2)}) collective-permute-start(f32[19,8,1,130]{3,2,1,0:T(1,128)S(1)} %get-tuple-element.198), channel_id=1, source_target_pairs={{0,1},{1,2},{2,3},{3,0},{4,5},{5,6},{6,7},{7,4},{8,9},{9,10},{10,1... | collective-permute-start | bytes 237128 | tf_op jit(solution)/shard_map/ppermute | solution.py:46
  76.1 0.7 copy-start.6
  76.1 0.8 copy-start.7
  76.1 0.8 copy-start.8
  76.1 0.8 copy-start.10
  76.1 0.8 copy-start.11
  76.9 0.7 copy-start.13
  78.3 0.7 copy-start.9
  79.6 0.7 copy-start.5
  81.3 0.7 copy-start.4
  82.0 0.7 copy-start.3
  123.8 0.7 copy-start.15
  127.1 5.9 %collective-permute-start.8 = (f32[19,8,8,1]{0,2,3,1:T(8,128)S(1)}, f32[19,8,8,1]{0,2,3,1:T(8,128)S(1)}, u32[]{:S(2)}, u32[]{:S(2)}) collective-permute-start(f32[19,8,8,1]{0,2,3,1:T(8,128)S(1)} %copy.88), channel_id=1, source_target_pairs={{0,4},{4,8},{8,12},{12,16},{16,20},{20,24},{24,28},{28,0},{1,5},{5... | collective-permute-start | bytes 14600 | tf_op jit(solution)/shard_map/ppermute | solution.py:46
  127.2 5.1 %collective-permute-start.9 = (f32[19,8,8,1]{0,2,3,1:T(8,128)S(1)}, f32[19,8,8,1]{0,2,3,1:T(8,128)S(1)}, u32[]{:S(2)}, u32[]{:S(2)}) collective-permute-start(f32[19,8,8,1]{0,2,3,1:T(8,128)S(1)} %copy.90), channel_id=1, source_target_pairs={{4,0},{8,4},{12,8},{16,12},{20,16},{24,20},{28,24},{0,28},{5,1},{9... | collective-permute-start | bytes 14600 | tf_op jit(solution)/shard_map/ppermute | solution.py:49
  133.8 4.7 %copy-start.2 = (f32[19,8,8,128]{3,2,1,0:T(8,128)S(1)}, f32[19,8,8,128]{3,2,1,0:T(8,128)}, u32[]{:S(2)}) copy-start(f32[19,8,8,128]{3,2,1,0:T(8,128)} %constant_dynamic-update-slice_fusion.115) | copy-start | bytes 1867780
  134.9 8.0 %collective-permute-start.11 = (f32[19,8,1,130]{3,2,1,0:T(1,128)S(1)}, f32[19,8,1,130]{3,2,1,0:T(1,128)S(1)}, u32[]{:S(2)}, u32[]{:S(2)}) collective-permute-start(f32[19,8,1,130]{3,2,1,0:T(1,128)S(1)} %get-tuple-element.193), channel_id=1, source_target_pairs={{1,0},{2,1},{3,2},{0,3},{5,4},{6,5},{7,6},{4,7},{9,8},{10,9},{11,1... | collective-permute-start | bytes 237128 | tf_op jit(solution)/shard_map/ppermute | solution.py:49
  138.5 7.2 %collective-permute-start.10 = (f32[19,8,1,130]{3,2,1,0:T(1,128)S(1)}, f32[19,8,1,130]{3,2,1,0:T(1,128)S(1)}, u32[]{:S(2)}, u32[]{:S(2)}) collective-permute-start(f32[19,8,1,130]{3,2,1,0:T(1,128)S(1)} %get-tuple-element.194), channel_id=1, source_target_pairs={{0,1},{1,2},{2,3},{3,0},{4,5},{5,6},{6,7},{7,4},{8,9},{9,10},{10,1... | collective-permute-start | bytes 237128 | tf_op jit(solution)/shard_map/ppermute | solution.py:46
  138.5 0.7 copy-start.16
  146.0 0.7 copy-start.17
  146.7 0.7 copy-start.18
  147.4 0.7 copy-start.21
  (2 other events, 1.4 us)
where the time goes:
time: 151 us; the launch traced here: 149 us
  blocking collectives  77.9 us (52%)
  starting transfers between devices  20.7 us (14%)
  local copies, waits for them, and re-layouts  17.8 us (12%)
  other arithmetic  14.9 us (10%)
  waiting for transfers between devices  14 us (9%)
  matrix products  2.11 us (1%)
  between operations  2.08 us (1%)
    psum x2, blocking collectives, total_flow(): return lax.psum(local_sum, ('gx', 'gz')) / node_total  77.9 us
    ppermute x6, starting transfers between devices, extended(): lax.ppermute(lax.slice_in_dim(block, 0, width, axis=dim), axis, backward)  18.6 us
    unnamed x55, local copies, waits for them, and re-layouts  8.54 us
    ppermute x6, waiting for transfers between devices, extended(): lax.ppermute(lax.slice_in_dim(block, block.shape[dim] - width, None, axis...  7.44 us
    ppermute x6, waiting for transfers between devices, extended(): lax.ppermute(lax.slice_in_dim(block, 0, width, axis=dim), axis, backward)  6.59 us
    unnamed x78, other arithmetic  6.22 us
    concatenate x5, other arithmetic, extended(): block = jnp.concatenate([low, block, high], axis=dim)  3.06 us
  transfers between devices with their start and end apart: 12, of which 6 were waited for; matrix products, arithmetic and copies ran while one was open for 8% of the time, Pallas kernels for 0%

commit v1 on v0

--- a/solution.py
+++ b/solution.py
@@ -35,6 +35,12 @@
 base_drive = 0.0001
 drive_gain = 1.0
 target_flow = 0.1
+
+
+def part_the_heads(incoming_x):
+    for d in ("gz", "gx"):
+        incoming_x = lax.psum(incoming_x, d)
+    return incoming_x
 
 
 def extended(block, sides, width):
@@ -211,7 +217,7 @@
 
 
 def total_flow(local_sum, node_total):
-    return lax.psum(local_sum, ("gx", "gz")) / node_total
+    return part_the_heads(local_sum) / node_total
 
 
 def local(populations, solid, top_inflow):

time: 151 us -> 117 us (0.77)
  blocking collectives: 77.9 us -> 50 us
  starting transfers between devices: 20.7 us -> 17.8 us
  waiting for transfers between devices: 14 us -> 11.4 us
    psum x2 -> x4, blocking collectives: 77.9 us -> 50 us  [part_the_heads(): incoming_x = lax.psum(incoming_x, d)]
    ppermute x6, starting transfers between devices: 18.6 us -> 14.2 us  [extended(): lax.ppermute(lax.slice_in_dim(block, 0, width, axis=dim), axis, backward)]
    ppermute x6, waiting for transfers between devices: 7.44 us -> 5.08 us  [extended(): lax.ppermute(lax.slice_in_dim(block, block.shape[dim] - width, None, axis...]
    ppermute x6, starting transfers between devices: 2.07 us -> 3.64 us  [extended(): lax.ppermute(lax.slice_in_dim(block, block.shape[dim] - width, None, axis...]
  transfers between devices with their start and end apart: 12 -> 12, of which waited for: 6 -> 7; matrix products, arithmetic and copies ran while one was open for 8% -> 10% of each run, Pallas kernels for 0% -> 0%
where the time goes in v1:
time: 117 us; the launch traced here: 116 us
  blocking collectives  50 us (43%)
  local copies, waits for them, and re-layouts  17.8 us (15%)
  starting transfers between devices  17.8 us (15%)
  other arithmetic  14.9 us (13%)
  waiting for transfers between devices  11.4 us (10%)
  matrix products  2.11 us (2%)
  between operations  2.08 us (2%)
    psum x4, blocking collectives, part_the_heads(): incoming_x = lax.psum(incoming_x, d)  50 us
    ppermute x6, starting transfers between devices, extended(): lax.ppermute(lax.slice_in_dim(block, 0, width, axis=dim), axis, backward)  14.2 us
    unnamed x55, local copies, waits for them, and re-layouts  8.54 us
    ppermute x6, waiting for transfers between devices, extended(): lax.ppermute(lax.slice_in_dim(block, 0, width, axis=dim), axis, backward)  6.28 us
    unnamed x78, other arithmetic  6.22 us
    ppermute x6, waiting for transfers between devices, extended(): lax.ppermute(lax.slice_in_dim(block, block.shape[dim] - width, None, axis...  5.08 us
    ppermute x6, starting transfers between devices, extended(): lax.ppermute(lax.slice_in_dim(block, block.shape[dim] - width, None, axis...  3.64 us
    concatenate x5, other arithmetic, extended(): block = jnp.concatenate([low, block, high], axis=dim)  3.03 us
  transfers between devices with their start and end apart: 12, of which 7 were waited for; matrix products, arithmetic and copies ran while one was open for 10% of the time, Pallas kernels for 0%

profile of v1, /device:TPU:0, one launch (start us, length us, event | category | flops | bytes accessed | tf_op | source)
XLA Modules:
  0.0 116.1 jit_solution(10198862536636841309)
XLA Ops:
  0.0 1.0 fusion.266
  1.0 4.5 %collective-permute-start.2 = (s32[8,8,1]{2,1,0:T(8,128)S(1)}, s32[8,8,1]{2,1,0:T(8,128)S(1)}, u32[]{:S(2)}, u32[]{:S(2)}) collective-permute-start(s32[8,8,1]{2,1,0:T(8,128)S(1)} %get-tuple-element.284), channel_id=1, source_target_pairs={{4,0},{8,4},{12,8},{16,12},{20,16},{24,20},{28,24},{0,28},{5,1},{9... | collective-permute-start | bytes 776 | tf_op jit(solution)/shard_map/ppermute | solution.py:55
  5.5 1.5 %fusion.243 = (f32[]{:T(128)}, f32[1,8,8,128]{3,2,1,0:T(8,128)S(1)}) fusion(s32[8,8,128]{2,1,0:T(8,128)S(1)} %copy-done.1, f32[19,8,8,128]{3,2,1,0:T(8,128)} %param.25), kind=kLoop, calls=%fused_computation.503 | loop fusion | flops 106495 | bytes 393220 | tf_op jit(solution)/shard_map/reduce_sum | solution.py:236
  7.0 10.5 %psum.28 = f32[]{:T(128)} all-reduce(f32[]{:T(128)} %get-tuple-element.179), channel_id=1, replica_groups=mesh['gx'=8,'gz'=4] {'gz'}, use_global_device_ids=true, to_apply=%region_2.0 | all-reduce | flops 1 | bytes 8 | tf_op jit(solution)/shard_map/psum | solution.py:42
  17.6 1.1 reduce_sum.40
  18.7 15.7 %psum.29 = f32[]{:T(128)} all-reduce(f32[]{:T(128)} %psum.28), channel_id=1, replica_groups=mesh['gx'=8,'gz'=4] {'gx'}, use_global_device_ids=true, to_apply=%region_3.0 | all-reduce | flops 1 | bytes 8 | tf_op jit(solution)/shard_map/psum | solution.py:42
  36.6 1.1 fusion.2
  38.1 1.2 copy.80
  39.8 3.6 %collective-permute-start.3 = (f32[19,8,8,1]{0,2,3,1:T(8,128)S(1)}, f32[19,8,8,1]{0,2,3,1:T(8,128)S(1)}, u32[]{:S(2)}, u32[]{:S(2)}) collective-permute-start(f32[19,8,8,1]{0,2,3,1:T(8,128)S(1)} %copy.82), channel_id=1, source_target_pairs={{4,0},{8,4},{12,8},{16,12},{20,16},{24,20},{28,24},{0,28},{5,1},{9... | collective-permute-start | bytes 14600 | tf_op jit(solution)/shard_map/ppermute | solution.py:55
  44.1 1.5 %collective-permute-start.4 = (s32[8,1,130]{2,1,0:T(1,128)S(1)}, s32[8,1,130]{2,1,0:T(1,128)S(1)}, u32[]{:S(2)}, u32[]{:S(2)}) collective-permute-start(s32[8,1,130]{2,1,0:T(1,128)S(1)} %get-tuple-element.243), channel_id=1, source_target_pairs={{0,1},{1,2},{2,3},{3,0},{4,5},{5,6},{6,7},{7,4},{8,9},{9,10},{10,1... | collective-permute-start | bytes 12488 | tf_op jit(solution)/shard_map/ppermute | solution.py:52
  45.7 0.7 pad_add_fusion.1
  46.4 0.7 fusion.265
  47.3 1.4 %collective-permute-done.4 = s32[8,1,130]{2,1,0:T(1,128)S(1)} collective-permute-done((s32[8,1,130]{2,1,0:T(1,128)S(1)}, s32[8,1,130]{2,1,0:T(1,128)S(1)}, u32[]{:S(2)}, u32[]{:S(2)}) %collective-permute-start.4) | collective-permute-done | bytes 4192 | tf_op jit(solution)/shard_map/ppermute | solution.py:52
  48.8 0.7 fusion.263
  50.3 1.5 %copy.81 = f32[19,8,8,1]{3,2,1,0:T(8,128)S(1)} copy(f32[19,8,8,1]{0,2,3,1:T(8,128)} %collective-permute-done.1) | data formatting | bytes 9728 | tf_op jit(solution)/shard_map/ppermute | solution.py:52
  51.9 1.0 pad_maximum_fusion.3
  54.3 1.4 %collective-permute-start.5 = (f32[19,8,1,130]{3,2,1,0:T(1,128)S(1)}, f32[19,8,1,130]{3,2,1,0:T(1,128)S(1)}, u32[]{:S(2)}, u32[]{:S(2)}) collective-permute-start(f32[19,8,1,130]{3,2,1,0:T(1,128)S(1)} %get-tuple-element.198), channel_id=1, source_target_pairs={{0,1},{1,2},{2,3},{3,0},{4,5},{5,6},{6,7},{7,4},{8,9},{9,10},{10,1... | collective-permute-start | bytes 237128 | tf_op jit(solution)/shard_map/ppermute | solution.py:52
  56.3 2.6 %collective-permute-done.7 = f32[19,8,1,130]{3,2,1,0:T(1,128)S(1)} collective-permute-done((f32[19,8,1,130]{3,2,1,0:T(1,128)S(1)}, f32[19,8,1,130]{3,2,1,0:T(1,128)S(1)}, u32[]{:S(2)}, u32[]{:S(2)}) %collective-permute-start.7) | collective-permute-done | bytes 79072 | tf_op jit(solution)/shard_map/ppermute | solution.py:55
  58.9 1.7 %collective-permute-done.5 = f32[19,8,1,130]{3,2,1,0:T(1,128)S(1)} collective-permute-done((f32[19,8,1,130]{3,2,1,0:T(1,128)S(1)}, f32[19,8,1,130]{3,2,1,0:T(1,128)S(1)}, u32[]{:S(2)}, u32[]{:S(2)}) %collective-permute-start.5) | collective-permute-done | bytes 79072 | tf_op jit(solution)/shard_map/ppermute | solution.py:52
  64.2 0.7 copy-done.5
  66.6 0.7 copy-done.3
  68.1 9.6 %psum.30 = f32[]{:T(128)} all-reduce(f32[]{:T(128)} %get-tuple-element.131), channel_id=1, replica_groups=mesh['gx'=8,'gz'=4] {'gz'}, use_global_device_ids=true, to_apply=%region_6.7 | all-reduce | flops 1 | bytes 8 | tf_op jit(solution)/shard_map/psum | solution.py:42
  77.6 14.2 %psum.31 = f32[]{:T(128)} all-reduce(f32[]{:T(128)} %psum.30), channel_id=1, replica_groups=mesh['gx'=8,'gz'=4] {'gx'}, use_global_device_ids=true, to_apply=%region_7.8 | all-reduce | flops 1 | bytes 8 | tf_op jit(solution)/shard_map/psum | solution.py:42
  94.0 1.1 fusion
  96.7 3.5 %collective-permute-start.9 = (f32[19,8,8,1]{0,2,3,1:T(8,128)S(1)}, f32[19,8,8,1]{0,2,3,1:T(8,128)S(1)}, u32[]{:S(2)}, u32[]{:S(2)}) collective-permute-start(f32[19,8,8,1]{0,2,3,1:T(8,128)S(1)} %copy.90), channel_id=1, source_target_pairs={{4,0},{8,4},{12,8},{16,12},{20,16},{24,20},{28,24},{0,28},{5,1},{9... | collective-permute-start | bytes 14600 | tf_op jit(solution)/shard_map/ppermute | solution.py:55
  100.8 1.0 collective-permute-done.9
  102.5 0.7 copy.89
  103.4 1.0 pad_maximum_fusion
  104.4 1.4 %collective-permute-start.11 = (f32[19,8,1,130]{3,2,1,0:T(1,128)S(1)}, f32[19,8,1,130]{3,2,1,0:T(1,128)S(1)}, u32[]{:S(2)}, u32[]{:S(2)}) collective-permute-start(f32[19,8,1,130]{3,2,1,0:T(1,128)S(1)} %get-tuple-element.193), channel_id=1, source_target_pairs={{1,0},{2,1},{3,2},{0,3},{5,4},{6,5},{7,6},{4,7},{9,8},{10,9},{11,1... | collective-permute-start | bytes 237128 | tf_op jit(solution)/shard_map/ppermute | solution.py:55
  107.9 2.5 %collective-permute-done.11 = f32[19,8,1,130]{3,2,1,0:T(1,128)S(1)} collective-permute-done((f32[19,8,1,130]{3,2,1,0:T(1,128)S(1)}, f32[19,8,1,130]{3,2,1,0:T(1,128)S(1)}, u32[]{:S(2)}, u32[]{:S(2)}) %collective-permute-start.11) | collective-permute-done | bytes 79072 | tf_op jit(solution)/shard_map/ppermute | solution.py:55
  110.4 2.0 %collective-permute-done.10 = f32[19,8,1,130]{3,2,1,0:T(1,128)S(1)} collective-permute-done((f32[19,8,1,130]{3,2,1,0:T(1,128)S(1)}, f32[19,8,1,130]{3,2,1,0:T(1,128)S(1)}, u32[]{:S(2)}, u32[]{:S(2)}) %collective-permute-start.10) | collective-permute-done | bytes 79072 | tf_op jit(solution)/shard_map/ppermute | solution.py:52
  115.1 0.9 broadcast_select_fusion
  (172 shorter events, 21.2 us)
Async XLA Ops:
  0.0 5.5 %copy-start.1 = (s32[8,8,128]{2,1,0:T(8,128)S(1)}, s32[8,8,128]{2,1,0:T(8,128)}, u32[]{:S(2)}) copy-start(s32[8,8,128]{2,1,0:T(8,128)} %param.26) | copy-start | bytes 98308
  0.0 35.1 %copy-start = (f32[19,8,8,128]{3,2,1,0:T(8,128)S(1)}, f32[19,8,8,128]{3,2,1,0:T(8,128)}, u32[]{:S(2)}) copy-start(f32[19,8,8,128]{3,2,1,0:T(8,128)} %param.25) | copy-start | bytes 1867780
  1.0 42.5 %collective-permute-start.2 = (s32[8,8,1]{2,1,0:T(8,128)S(1)}, s32[8,8,1]{2,1,0:T(8,128)S(1)}, u32[]{:S(2)}, u32[]{:S(2)}) collective-permute-start(s32[8,8,1]{2,1,0:T(8,128)S(1)} %get-tuple-element.284), channel_id=1, source_target_pairs={{4,0},{8,4},{12,8},{16,12},{20,16},{24,20},{28,24},{0,28},{5,1},{9... | collective-permute-start | bytes 776 | tf_op jit(solution)/shard_map/ppermute | solution.py:55
  5.5 37.9 %collective-permute-start = (s32[8,8,1]{2,1,0:T(8,128)S(1)}, s32[8,8,1]{2,1,0:T(8,128)S(1)}, u32[]{:S(2)}, u32[]{:S(2)}) collective-permute-start(s32[8,8,1]{2,1,0:T(8,128)S(1)} %get-tuple-element.285), channel_id=1, source_target_pairs={{0,4},{4,8},{8,12},{12,16},{16,20},{20,24},{24,28},{28,0},{1,5},{5... | collective-permute-start | bytes 776 | tf_op jit(solution)/shard_map/ppermute | solution.py:52
  35.9 0.7 copy-start.14
  39.3 11.0 %collective-permute-start.1 = (f32[19,8,8,1]{0,2,3,1:T(8,128)}, f32[19,8,8,1]{0,2,3,1:T(8,128)}, u32[]{:S(2)}, u32[]{:S(2)}) collective-permute-start(f32[19,8,8,1]{0,2,3,1:T(8,128)} %copy.80), channel_id=1, source_target_pairs={{0,4},{4,8},{8,12},{12,16},{16,20},{20,24},{24,28},{28,0},{1,5},{5... | collective-permute-start | bytes 14600 | tf_op jit(solution)/shard_map/ppermute | solution.py:52
  39.8 9.7 %collective-permute-start.3 = (f32[19,8,8,1]{0,2,3,1:T(8,128)S(1)}, f32[19,8,8,1]{0,2,3,1:T(8,128)S(1)}, u32[]{:S(2)}, u32[]{:S(2)}) collective-permute-start(f32[19,8,8,1]{0,2,3,1:T(8,128)S(1)} %copy.82), channel_id=1, source_target_pairs={{4,0},{8,4},{12,8},{16,12},{20,16},{24,20},{28,24},{0,28},{5,1},{9... | collective-permute-start | bytes 14600 | tf_op jit(solution)/shard_map/ppermute | solution.py:55
  43.6 3.7 %collective-permute-start.6 = (s32[8,1,130]{2,1,0:T(1,128)S(1)}, s32[8,1,130]{2,1,0:T(1,128)S(1)}, u32[]{:S(2)}, u32[]{:S(2)}) collective-permute-start(s32[8,1,130]{2,1,0:T(1,128)S(1)} %get-tuple-element.242), channel_id=1, source_target_pairs={{1,0},{2,1},{3,2},{0,3},{5,4},{6,5},{7,6},{4,7},{9,8},{10,9},{11,1... | collective-permute-start | bytes 12488 | tf_op jit(solution)/shard_map/ppermute | solution.py:55
  44.1 4.5 %collective-permute-start.4 = (s32[8,1,130]{2,1,0:T(1,128)S(1)}, s32[8,1,130]{2,1,0:T(1,128)S(1)}, u32[]{:S(2)}, u32[]{:S(2)}) collective-permute-start(s32[8,1,130]{2,1,0:T(1,128)S(1)} %get-tuple-element.243), channel_id=1, source_target_pairs={{0,1},{1,2},{2,3},{3,0},{4,5},{5,6},{6,7},{7,4},{8,9},{9,10},{10,1... | collective-permute-start | bytes 12488 | tf_op jit(solution)/shard_map/ppermute | solution.py:52
  53.0 2.7 %copy-start.12 = (s32[7,8,128]{2,1,0:T(8,128)S(1)}, s32[7,8,128]{2,1,0:T(8,128)}, u32[]{:S(2)}) copy-start(s32[7,8,128]{2,1,0:T(8,128)} %get-tuple-element.282) | copy-start | bytes 86020
  53.7 5.2 %collective-permute-start.7 = (f32[19,8,1,130]{3,2,1,0:T(1,128)S(1)}, f32[19,8,1,130]{3,2,1,0:T(1,128)S(1)}, u32[]{:S(2)}, u32[]{:S(2)}) collective-permute-start(f32[19,8,1,130]{3,2,1,0:T(1,128)S(1)} %get-tuple-element.197), channel_id=1, source_target_pairs={{1,0},{2,1},{3,2},{0,3},{5,4},{6,5},{7,6},{4,7},{9,8},{10,9},{11,1... | collective-permute-start | bytes 237128 | tf_op jit(solution)/shard_map/ppermute | solution.py:55
  54.3 6.3 %collective-permute-start.5 = (f32[19,8,1,130]{3,2,1,0:T(1,128)S(1)}, f32[19,8,1,130]{3,2,1,0:T(1,128)S(1)}, u32[]{:S(2)}, u32[]{:S(2)}) collective-permute-start(f32[19,8,1,130]{3,2,1,0:T(1,128)S(1)} %get-tuple-element.198), channel_id=1, source_target_pairs={{0,1},{1,2},{2,3},{3,0},{4,5},{5,6},{6,7},{7,4},{8,9},{9,10},{10,1... | collective-permute-start | bytes 237128 | tf_op jit(solution)/shard_map/ppermute | solution.py:52
  60.6 0.7 copy-start.6
  60.6 0.8 copy-start.7
  60.6 0.8 copy-start.8
  60.6 0.8 copy-start.10
  60.6 0.8 copy-start.11
  61.4 0.7 copy-start.13
  62.9 0.7 copy-start.9
  64.2 0.7 copy-start.5
  65.8 0.7 copy-start.4
  66.6 0.7 copy-start.3
  93.3 0.7 copy-start.15
  96.6 5.9 %collective-permute-start.8 = (f32[19,8,8,1]{0,2,3,1:T(8,128)S(1)}, f32[19,8,8,1]{0,2,3,1:T(8,128)S(1)}, u32[]{:S(2)}, u32[]{:S(2)}) collective-permute-start(f32[19,8,8,1]{0,2,3,1:T(8,128)S(1)} %copy.88), channel_id=1, source_target_pairs={{0,4},{4,8},{8,12},{12,16},{16,20},{20,24},{24,28},{28,0},{1,5},{5... | collective-permute-start | bytes 14600 | tf_op jit(solution)/shard_map/ppermute | solution.py:52
  96.7 5.1 %collective-permute-start.9 = (f32[19,8,8,1]{0,2,3,1:T(8,128)S(1)}, f32[19,8,8,1]{0,2,3,1:T(8,128)S(1)}, u32[]{:S(2)}, u32[]{:S(2)}) collective-permute-start(f32[19,8,8,1]{0,2,3,1:T(8,128)S(1)} %copy.90), channel_id=1, source_target_pairs={{4,0},{8,4},{12,8},{16,12},{20,16},{24,20},{28,24},{0,28},{5,1},{9... | collective-permute-start | bytes 14600 | tf_op jit(solution)/shard_map/ppermute | solution.py:55
  103.4 3.1 %copy-start.2 = (f32[19,8,8,128]{3,2,1,0:T(8,128)S(1)}, f32[19,8,8,128]{3,2,1,0:T(8,128)}, u32[]{:S(2)}) copy-start(f32[19,8,8,128]{3,2,1,0:T(8,128)} %constant_dynamic-update-slice_fusion.115) | copy-start | bytes 1867780
  104.4 6.0 %collective-permute-start.11 = (f32[19,8,1,130]{3,2,1,0:T(1,128)S(1)}, f32[19,8,1,130]{3,2,1,0:T(1,128)S(1)}, u32[]{:S(2)}, u32[]{:S(2)}) collective-permute-start(f32[19,8,1,130]{3,2,1,0:T(1,128)S(1)} %get-tuple-element.193), channel_id=1, source_target_pairs={{1,0},{2,1},{3,2},{0,3},{5,4},{6,5},{7,6},{4,7},{9,8},{10,9},{11,1... | collective-permute-start | bytes 237128 | tf_op jit(solution)/shard_map/ppermute | solution.py:55
  105.8 6.6 %collective-permute-start.10 = (f32[19,8,1,130]{3,2,1,0:T(1,128)S(1)}, f32[19,8,1,130]{3,2,1,0:T(1,128)S(1)}, u32[]{:S(2)}, u32[]{:S(2)}) collective-permute-start(f32[19,8,1,130]{3,2,1,0:T(1,128)S(1)} %get-tuple-element.194), channel_id=1, source_target_pairs={{0,1},{1,2},{2,3},{3,0},{4,5},{5,6},{6,7},{7,4},{8,9},{9,10},{10,1... | collective-permute-start | bytes 237128 | tf_op jit(solution)/shard_map/ppermute | solution.py:52
  106.5 0.7 copy-start.16
  107.2 0.7 copy-start.19
  112.5 0.7 copy-start.17
  113.9 0.7 copy-start.21
  (2 other events, 1.4 us)
